TPU v7x, 32 devices: a whole 2x2x4 slice. The times are simulated.
32 devices in a mesh: row: 4 (over y, core), col: 8 (over z, x).
Axes of the slice: x: 2, y: 2, z: 4, core: 2. Of those that a mesh axis runs over, the one named last changes fastest.
Arguments:
- vectors: bfloat16 [4, 8, 128, 384], P('row', 'col'), may hold values from -6 to 6
- near_blocks: bfloat16 [4, 8, 9, 384, 384], P('row', 'col'), may hold values from -0.15625 to 0.15625
- near_source: int32 [4, 8, 9], P('row', 'col'), may hold values from 0 to 8, each once within a row
- near_count: int32 [4, 8], P('row', 'col'), may hold values from 1 to 9
- basis_col: bfloat16 [4, 8, 64, 384], P('row', 'col'), may hold values from -0.3125 to 0.3125
- transfer_col: bfloat16 [4, 8, 64, 64], P('row', 'col'), may hold values from -0.25 to 0.25
- leaf_couple: bfloat16 [4, 8, 3, 5, 64, 64], P('row', 'col'), may hold values from -0.1875 to 0.1875
- coupling: bfloat16 [4, 4, 64, 64], P('row'), may hold values from -0.75 to 0.75
- distant_region_list: int32 [4, 4], P('row'), may hold values from 0 to 3, each once within a row
- transfer_row: bfloat16 [4, 8, 64, 64], P('row', 'col'), may hold values from -0.75 to 0.75
- basis_row: bfloat16 [4, 8, 64, 384], P('row', 'col'), may hold values from -0.75 to 0.75
Outputs:
- product: bfloat16 [4, 8, 128, 384], P('row', 'col')
Inputs may be any that keep to these rules, and one draw needn't show every extreme that they name: `near_source`: the 9 slots of a leaf name the nine neighbourhood cells once each. Only the first near_count slots of a leaf are live. `distant_region_list`: each region's list names every region once.
All inputs are finite; a program needn't handle non-finite values.
Results may differ from a plain program's by a relative error of at most 0.013.
Values may be sent and summed in bfloat16 or wider, within the bound.
A program may use at most 64 MiB of HBM per device.

v0:
```python
import jax
import jax.numpy as jnp
from jax import lax
from jax.sharding import PartitionSpec as P


def from_behind(value, axis, steps):
    count = lax.axis_size(axis)
    pairs = [(source, (source + steps) % count) for source in range(count)]
    return lax.ppermute(value, axis, pairs)


def padded_2(cells, sides, width):
    for axis, dim in sides:
        count = lax.axis_size(axis)
        head = lax.slice_in_dim(cells, 0, width, axis=dim)
        tail = lax.slice_in_dim(cells, cells.shape[dim] - width, cells.shape[dim], axis=dim)
        cells = jnp.concatenate(
            [
                lax.ppermute(tail, axis, [(i, (i + 1) % count) for i in range(count)]),
                cells,
                lax.ppermute(head, axis, [((i + 1) % count, i) for i in range(count)]),
            ],
            axis=dim,
        )
    return cells


def per_device(
    vectors,
    near_blocks,
    near_source,
    near_count,
    basis_col,
    transfer_col,
    leaf_couple,
    coupling,
    distant_region_list,
    transfer_row,
    basis_row,
):
    upper_limit = lax.Precision.HIGHEST
    leading = from_behind(vectors, "row", -1)
    leading = from_behind(leading, "col", -1)
    padded = padded_2(leading, (("row", 0), ("col", 1)), 1)
    table = padded.reshape(9, padded.shape[2], padded.shape[3])
    picked = jnp.take(table, near_source[0, 0], axis=0)
    slots = jnp.arange(picked.shape[0], dtype=jnp.int32)
    live_mask = (slots < near_count[0, 0])[:, None, None]
    picked = jnp.where(live_mask, picked, jnp.zeros_like(picked))
    near_part = jnp.einsum(
        "svp,spq->vq", picked, near_blocks[0, 0], preferred_element_type=jnp.float32
    )
    incoming_leaf = lax.dot_general(
        vectors[0, 0], basis_col[0, 0], (((1,), (1,)), ((), ())), preferred_element_type=jnp.float32
    )
    next_row = from_behind(incoming_leaf.astype(jnp.bfloat16), "row", -1).astype(
        incoming_leaf.dtype
    )
    second_row = from_behind(incoming_leaf.astype(jnp.bfloat16), "row", -2).astype(
        incoming_leaf.dtype
    )
    three_rows = jnp.stack([incoming_leaf, next_row, second_row], axis=0)
    leaves_of_rows = lax.all_gather(
        three_rows[:, None].astype(jnp.bfloat16), "col", axis=1, tiled=True
    ).astype(jnp.float32)
    col_count = lax.axis_size("col")
    rolled = jnp.roll(leaves_of_rows, -(lax.axis_index("col") + 3), axis=1)[:, : col_count - 3]
    band = jnp.einsum(
        "dfvk,dfkl->vl", rolled, leaf_couple[0, 0].astype(jnp.float32), precision=upper_limit
    )
    upward = jnp.dot(incoming_leaf, transfer_col[0, 0].astype(jnp.float32), precision=upper_limit)
    row_count = lax.axis_size("row")
    own_region = lax.psum(upward.astype(jnp.bfloat16), "col").astype(jnp.float32)
    regions = lax.all_gather(
        own_region[None].astype(jnp.bfloat16), "row", axis=0, tiled=True
    ).astype(jnp.float32)
    listing = distant_region_list[0]
    far_mask = ((listing - lax.axis_index("row")) % row_count >= 3).astype(jnp.float32)
    far_coeff = jnp.take(regions, listing, axis=0) * far_mask[:, None, None]
    outgoing_region = jnp.einsum(
        "fvk,fkl->vl", far_coeff, coupling[0].astype(jnp.float32), precision=upper_limit
    )
    leaf_out = band + jnp.dot(
        outgoing_region, transfer_row[0, 0].astype(jnp.float32), precision=upper_limit
    )
    far_part = jnp.dot(leaf_out, basis_row[0, 0].astype(jnp.float32), precision=upper_limit)
    return (near_part + far_part).astype(jnp.bfloat16)[None, None]


def solution(mesh):
    placed = (
        P("row", "col", None, None),
        P("row", "col", None, None, None),
        P("row", "col", None),
        P("row", "col"),
        P("row", "col", None, None),
        P("row", "col", None, None),
        P("row", "col", None, None, None, None),
        P("row", None, None, None),
        P("row", None),
        P("row", "col", None, None),
        P("row", "col", None, None),
    )
    return jax.shard_map(
        per_device,
        mesh=mesh,
        in_specs=placed,
        out_specs=P("row", "col", None, None),
        check_vma=False,
    )
```

profile of v0, /device:TPU:1, one launch (start us, length us, event | category | flops | bytes accessed | tf_op | source)
XLA Modules:
  0.0 112.0 jit_solution(17042163950172736035)
XLA Ops:
  0.0 0.0 copy-start
  0.0 0.0 copy-start.3
  0.0 0.0 collective-permute-start
  0.0 1.2 %fusion.37 = (bf16[128,64]{0,1:T(8,128)(2,1)S(1)}, f32[128,64]{0,1:T(8,128)S(1)}) fusion(bf16[1,1,64,384]{3,2,1,0:T(8,128)(2,1)} %param.15, bf16[1,1,128,384]{3,2,1,0:T(8,128)(2,1)} %param.11), kind=kOutput, calls=%fused_computation.62 | convolution fusion | flops 6299648 | bytes 196608 | tf_op jit(solution)/shard_map/dot_general | solution.py:54
  1.2 2.7 %collective-permute-start.7 = (bf16[128,64]{0,1:T(8,128)(2,1)S(1)}, bf16[128,64]{0,1:T(8,128)(2,1)S(1)}, u32[]{:S(2)}, u32[]{:S(2)}) collective-permute-start(bf16[128,64]{0,1:T(8,128)(2,1)S(1)} %get-tuple-element.7), channel_id=1, source_target_pairs={{0,16},{8,24},{16,0},{24,8},{1,17},{9,25},{17,1},{25,9},{2,18},{10... | collective-permute-start | bytes 49160 | tf_op jit(solution)/shard_map/ppermute | solution.py:10
  4.0 0.3 collective-permute-start.6
  4.3 0.7 fusion.30
  5.6 0.7 compare_and_fusion.1
  6.3 0.9 fusion.7
  7.2 30.1 %psum.7 = bf16[1,128,64]{1,2,0:T(8,128)(2,1)S(1)} all-reduce(bf16[1,128,64]{1,2,0:T(8,128)(2,1)S(1)} %fusion.7), channel_id=1, replica_groups=mesh['row'=4,'col'=8] {'col'}, use_global_device_ids=true, to_apply=%region_0.1 | all-reduce | flops 8192 | bytes 32768 | tf_op jit(solution)/shard_map/psum | solution.py:74
  37.4 12.6 %all_gather.7 = bf16[4,128,64]{1,2,0:T(8,128)(2,1)S(1)} all-gather(bf16[1,128,64]{1,2,0:T(8,128)(2,1)S(1)} %psum.7), channel_id=1, replica_groups=mesh['row'=4,'col'=8] {'row'}, dimensions={0}, use_global_device_ids=true | all-gather | bytes 81920 | tf_op jit(solution)/shard_map/all_gather | solution.py:75
  50.0 0.7 fusion.31
  50.6 0.7 compare_and_fusion
  51.3 0.6 gather_fusion.1
  51.9 1.2 %convolution_bitcast_fusion = f32[128,64]{1,0:T(8,128)S(1)} fusion(f32[4,128,64]{1,2,0:T(8,128)S(1)} %gather_fusion.1, bf16[1,4,64,64]{3,2,1,0:T(8,128)(2,1)} %param.18, f32[4]{0:T(128)S(1)} %get-tuple-element.6, pred[4]{0:T(512)(128)(4,1)S(1)} %get-tuple-element.5), kind=kOutput, calls=%fused_computation.9 | convolution fusion | flops 25231360 | bytes 196628 | tf_op jit(solution)/shard_map/fvk,fkl->vl/dot_general | solution.py:81
  53.1 0.0 collective-permute-done
  53.1 0.1 collective-permute-start.1
  53.2 0.0 collective-permute-done.7
  53.2 0.0 collective-permute-done.6
  53.2 4.1 %collective-permute-done.1 = bf16[1,1,128,384]{3,2,1,0:T(8,128)(2,1)S(1)} collective-permute-done((bf16[1,1,128,384]{3,2,1,0:T(8,128)(2,1)S(1)}, bf16[1,1,128,384]{3,2,1,0:T(8,128)(2,1)S(1)}, u32[]{:S(2)}, u32[]{:S(2)}) %collective-permute-start.1) | collective-permute-done | bytes 98336 | tf_op jit(solution)/shard_map/ppermute | solution.py:10
  57.4 2.1 %collective-permute-start.2 = (bf16[1,1,128,384]{3,2,1,0:T(8,128)(2,1)S(1)}, bf16[1,1,128,384]{3,2,1,0:T(8,128)(2,1)S(1)}, u32[]{:S(2)}, u32[]{:S(2)}) collective-permute-start(bf16[1,1,128,384]{3,2,1,0:T(8,128)(2,1)S(1)} %collective-permute-done.1), channel_id=1, source_target_pairs={{0,8},{8,16},{16,24},{24,0},{1,9},{9,17},{17,25},{25,1},{2,10},{10... | collective-permute-start | bytes 294920 | tf_op jit(solution)/shard_map/ppermute | solution.py:20
  59.5 25.3 %all_gather.6 = bf16[3,8,128,64]{2,3,1,0:T(8,128)(2,1)S(1)} all-gather(bf16[3,1,128,64]{2,3,1,0:T(8,128)(2,1)S(1)} %pad_maximum_fusion.1), channel_id=1, replica_groups=mesh['row'=4,'col'=8] {'col'}, dimensions={1}, use_global_device_ids=true | all-gather | bytes 442368 | tf_op jit(solution)/shard_map/all_gather | solution.py:64
  84.8 4.8 %collective-permute-start.3 = (bf16[1,1,128,384]{3,2,1,0:T(8,128)(2,1)S(1)}, bf16[1,1,128,384]{3,2,1,0:T(8,128)(2,1)S(1)}, u32[]{:S(2)}, u32[]{:S(2)}) collective-permute-start(bf16[1,1,128,384]{3,2,1,0:T(8,128)(2,1)S(1)} %collective-permute-done.1), channel_id=1, source_target_pairs={{8,0},{16,8},{24,16},{0,24},{9,1},{17,9},{25,17},{1,25},{10,2},{18... | collective-permute-start | bytes 294920 | tf_op jit(solution)/shard_map/ppermute | solution.py:22
  89.6 0.0 collective-permute-done.2
  89.6 3.4 %collective-permute-done.3 = bf16[1,1,128,384]{3,2,1,0:T(8,128)(2,1)S(1)} collective-permute-done((bf16[1,1,128,384]{3,2,1,0:T(8,128)(2,1)S(1)}, bf16[1,1,128,384]{3,2,1,0:T(8,128)(2,1)S(1)}, u32[]{:S(2)}, u32[]{:S(2)}) %collective-permute-start.3) | collective-permute-done | bytes 98336 | tf_op jit(solution)/shard_map/ppermute | solution.py:22
  93.0 2.5 %collective-permute-start.5 = (bf16[3,1,128,384]{3,2,1,0:T(8,128)(2,1)S(1)}, bf16[3,1,128,384]{3,2,1,0:T(8,128)(2,1)S(1)}, u32[]{:S(2)}, u32[]{:S(2)}) collective-permute-start(bf16[3,1,128,384]{3,2,1,0:T(8,128)(2,1)S(1)} %constant_dynamic-update-slice_fusion), channel_id=1, source_target_pairs={{1,0},{2,1},{3,2},{4,3},{5,4},{6,5},{7,6},{0,7},{9,8},{10,9},{11,1... | collective-permute-start | bytes 884744 | tf_op jit(solution)/shard_map/ppermute | solution.py:22
  95.5 0.0 collective-permute-start.4
  95.5 1.2 %convolution_bitcast_fusion.1 = f32[128,64]{1,0:T(8,128)S(1)} fusion(s32[]{:T(128)S(6)} %select_n.72, bf16[3,8,128,64]{2,3,1,0:T(8,128)(2,1)S(1)} %all_gather.6, bf16[1,1,3,5,64,64]{5,4,3,2,1,0:T(8,128)(2,1)} %param.17), kind=kOutput, calls=%fused_computation.10 | convolution fusion | flops 16515072 | bytes 548868 | tf_op jit(solution)/shard_map/dfvk,dfkl->vl/dot_general | solution.py:69
  96.7 0.0 copy-done.3
  96.8 0.8 convolution_add_fusion.1
  97.5 9.9 %collective-permute-done.5 = bf16[3,1,128,384]{3,2,1,0:T(8,128)(2,1)S(1)} collective-permute-done((bf16[3,1,128,384]{3,2,1,0:T(8,128)(2,1)S(1)}, bf16[3,1,128,384]{3,2,1,0:T(8,128)(2,1)S(1)}, u32[]{:S(2)}, u32[]{:S(2)}) %collective-permute-start.5) | collective-permute-done | bytes 294944 | tf_op jit(solution)/shard_map/ppermute | solution.py:22
  107.4 0.0 collective-permute-done.4
  107.4 0.1 pad_maximum_fusion
  107.5 1.7 %gather_fusion = bf16[9,128,384]{2,1,0:T(8,128)(2,1)} fusion(bf16[9,128,384]{2,1,0:T(8,128)(2,1)S(1)} %bitcast.66, s32[1024]{0:T(1024)S(1)} %pad_clamp_fusion.1), kind=kCustom, calls=%fused_computation | custom fusion | bytes 1769508 | tf_op jit(solution)/shard_map/jit(_take)/gather | solution.py:47
  109.2 0.0 copy-start.1
  109.2 0.0 copy-start.2
  109.2 0.0 copy-done
  109.2 1.9 %fusion.2 = f32[128,384]{1,0:T(8,128)S(1)} fusion(bf16[1,1,9,384,384]{4,3,2,1,0:T(8,128)(2,1)S(1)} %copy-done, bf16[9,128,384]{2,1,0:T(8,128)(2,1)} %gather_fusion, pred[9]{0:T(512)(128)(4,1)S(1)} %get-tuple-element.9, pred[9]{0:T(512)(128)(4,1)S(1)} %get-tuple-element.10), kind=kOutput, calls=%fused_computation.5 | convolution fusion | flops 340623360 | bytes 3735570 | tf_op jit(solution)/shard_map/svp,spq->vq/dot_general | solution.py:51
  111.1 0.0 copy-done.1
  111.1 0.0 copy-done.2
  111.1 0.9 fusion.6
  (7 shorter events, 0.1 us)
Async XLA Ops:
  0.0 109.2 %copy-start = (bf16[1,1,9,384,384]{4,3,2,1,0:T(8,128)(2,1)S(1)}, bf16[1,1,9,384,384]{4,3,2,1,0:T(8,128)(2,1)}, u32[]{:S(2)}) copy-start(bf16[1,1,9,384,384]{4,3,2,1,0:T(8,128)(2,1)} %param.12) | copy-start | bytes 7962628
  0.0 96.7 %copy-start.3 = (bf16[1,1,64,64]{3,2,1,0:T(8,128)(2,1)S(1)}, bf16[1,1,64,64]{3,2,1,0:T(8,128)(2,1)}, u32[]{:S(2)}) copy-start(bf16[1,1,64,64]{3,2,1,0:T(8,128)(2,1)} %param.20) | copy-start | bytes 24580
  0.0 53.1 %collective-permute-start = (bf16[1,1,128,384]{3,2,1,0:T(8,128)(2,1)}, bf16[1,1,128,384]{3,2,1,0:T(8,128)(2,1)S(1)}, u32[]{:S(2)}, u32[]{:S(2)}) collective-permute-start(bf16[1,1,128,384]{3,2,1,0:T(8,128)(2,1)} %param.11), channel_id=1, source_target_pairs={{0,24},{8,0},{16,8},{24,16},{1,25},{9,1},{17,9},{25,17},{2,26},{10... | collective-permute-start | bytes 294920 | tf_op jit(solution)/shard_map/ppermute | solution.py:10
  1.2 52.0 %collective-permute-start.7 = (bf16[128,64]{0,1:T(8,128)(2,1)S(1)}, bf16[128,64]{0,1:T(8,128)(2,1)S(1)}, u32[]{:S(2)}, u32[]{:S(2)}) collective-permute-start(bf16[128,64]{0,1:T(8,128)(2,1)S(1)} %get-tuple-element.7), channel_id=1, source_target_pairs={{0,16},{8,24},{16,0},{24,8},{1,17},{9,25},{17,1},{25,9},{2,18},{10... | collective-permute-start | bytes 49160 | tf_op jit(solution)/shard_map/ppermute | solution.py:10
  4.0 49.2 %collective-permute-start.6 = (bf16[128,64]{0,1:T(8,128)(2,1)S(1)}, bf16[128,64]{0,1:T(8,128)(2,1)S(1)}, u32[]{:S(2)}, u32[]{:S(2)}) collective-permute-start(bf16[128,64]{0,1:T(8,128)(2,1)S(1)} %get-tuple-element.7), channel_id=1, source_target_pairs={{0,24},{8,0},{16,8},{24,16},{1,25},{9,1},{17,9},{25,17},{2,26},{10... | collective-permute-start | bytes 49160 | tf_op jit(solution)/shard_map/ppermute | solution.py:10
  53.1 4.2 %collective-permute-start.1 = (bf16[1,1,128,384]{3,2,1,0:T(8,128)(2,1)S(1)}, bf16[1,1,128,384]{3,2,1,0:T(8,128)(2,1)S(1)}, u32[]{:S(2)}, u32[]{:S(2)}) collective-permute-start(bf16[1,1,128,384]{3,2,1,0:T(8,128)(2,1)S(1)} %collective-permute-done), channel_id=1, source_target_pairs={{0,7},{1,0},{2,1},{3,2},{4,3},{5,4},{6,5},{7,6},{8,15},{9,8},{10,9... | collective-permute-start | bytes 294920 | tf_op jit(solution)/shard_map/ppermute | solution.py:10
  57.4 32.2 %collective-permute-start.2 = (bf16[1,1,128,384]{3,2,1,0:T(8,128)(2,1)S(1)}, bf16[1,1,128,384]{3,2,1,0:T(8,128)(2,1)S(1)}, u32[]{:S(2)}, u32[]{:S(2)}) collective-permute-start(bf16[1,1,128,384]{3,2,1,0:T(8,128)(2,1)S(1)} %collective-permute-done.1), channel_id=1, source_target_pairs={{0,8},{8,16},{16,24},{24,0},{1,9},{9,17},{17,25},{25,1},{2,10},{10... | collective-permute-start | bytes 294920 | tf_op jit(solution)/shard_map/ppermute | solution.py:20
  84.8 8.2 %collective-permute-start.3 = (bf16[1,1,128,384]{3,2,1,0:T(8,128)(2,1)S(1)}, bf16[1,1,128,384]{3,2,1,0:T(8,128)(2,1)S(1)}, u32[]{:S(2)}, u32[]{:S(2)}) collective-permute-start(bf16[1,1,128,384]{3,2,1,0:T(8,128)(2,1)S(1)} %collective-permute-done.1), channel_id=1, source_target_pairs={{8,0},{16,8},{24,16},{0,24},{9,1},{17,9},{25,17},{1,25},{10,2},{18... | collective-permute-start | bytes 294920 | tf_op jit(solution)/shard_map/ppermute | solution.py:22
  93.0 14.4 %collective-permute-start.5 = (bf16[3,1,128,384]{3,2,1,0:T(8,128)(2,1)S(1)}, bf16[3,1,128,384]{3,2,1,0:T(8,128)(2,1)S(1)}, u32[]{:S(2)}, u32[]{:S(2)}) collective-permute-start(bf16[3,1,128,384]{3,2,1,0:T(8,128)(2,1)S(1)} %constant_dynamic-update-slice_fusion), channel_id=1, source_target_pairs={{1,0},{2,1},{3,2},{4,3},{5,4},{6,5},{7,6},{0,7},{9,8},{10,9},{11,1... | collective-permute-start | bytes 884744 | tf_op jit(solution)/shard_map/ppermute | solution.py:22
  95.5 11.9 %collective-permute-start.4 = (bf16[3,1,128,384]{3,2,1,0:T(8,128)(2,1)S(1)}, bf16[3,1,128,384]{3,2,1,0:T(8,128)(2,1)S(1)}, u32[]{:S(2)}, u32[]{:S(2)}) collective-permute-start(bf16[3,1,128,384]{3,2,1,0:T(8,128)(2,1)S(1)} %constant_dynamic-update-slice_fusion), channel_id=1, source_target_pairs={{0,1},{1,2},{2,3},{3,4},{4,5},{5,6},{6,7},{7,0},{8,9},{9,10},{10,1... | collective-permute-start | bytes 884744 | tf_op jit(solution)/shard_map/ppermute | solution.py:20
  109.2 1.9 %copy-start.1 = (f32[128,64]{1,0:T(8,128)S(1)}, f32[128,64]{1,0:T(8,128)}, u32[]{:S(2)}) copy-start(f32[128,64]{1,0:T(8,128)} %convolution_add_fusion.1) | copy-start | bytes 98308
  109.2 1.9 %copy-start.2 = (bf16[1,1,64,384]{3,2,1,0:T(8,128)(2,1)S(1)}, bf16[1,1,64,384]{3,2,1,0:T(8,128)(2,1)}, u32[]{:S(2)}) copy-start(bf16[1,1,64,384]{3,2,1,0:T(8,128)(2,1)} %param.21) | copy-start | bytes 147460
where the time goes:
time: 112 us
  blocking collectives  68.1 us (61%)
  waiting for transfers between devices  17.4 us (16%)
  starting transfers between devices  12.5 us (11%)
  matrix products  8.11 us (7%)
  other arithmetic  2.8 us (2%)
  local copies, waits for them, and re-layouts  2.28 us (2%)
    psum x1, blocking collectives, per_device(): lax.psum(upward.astype(jnp.bfloat16), 'col').astype(jnp.float32)  30.1 us
    all_gather x1, blocking collectives, per_device(): lax.all_gather(three_rows[:, None].astype(jnp.bfloat16), 'col', axis=1, t...  25.3 us
    ppermute x2, waiting for transfers between devices, padded_2(): lax.ppermute(head, axis, [((i + 1) % count, i) for i in range(count)])  13.2 us
    all_gather x1, blocking collectives, per_device(): lax.all_gather(own_region[None].astype(jnp.bfloat16), 'row', axis=0, tile...  12.6 us
    ppermute x2, starting transfers between devices, padded_2(): lax.ppermute(head, axis, [((i + 1) % count, i) for i in range(count)])  7.24 us
    ppermute x4, waiting for transfers between devices, from_behind(): return lax.ppermute(value, axis, pairs)  4.15 us
    ppermute x4, starting transfers between devices, from_behind(): return lax.ppermute(value, axis, pairs)  3.15 us
  transfers between devices with their start and end apart: 8, of which 3 were waited for; matrix products, arithmetic and copies ran while one was open for 8% of the time, Pallas kernels for 0%

commit v1 on v0

--- a/solution.py
+++ b/solution.py
@@ -71,7 +71,9 @@
     )
     upward = jnp.dot(incoming_leaf, transfer_col[0, 0].astype(jnp.float32), precision=upper_limit)
     row_count = lax.axis_size("row")
-    own_region = lax.psum(upward.astype(jnp.bfloat16), "col").astype(jnp.float32)
+    own_region = jnp.sum(lax.all_gather(upward.astype(jnp.bfloat16), "col"), axis=0).astype(
+        jnp.float32
+    )
     regions = lax.all_gather(
         own_region[None].astype(jnp.bfloat16), "row", axis=0, tiled=True
     ).astype(jnp.float32)

time: 112 us -> 103 us (0.920)
  blocking collectives: 68.1 us -> 57.8 us
  starting transfers between devices: 12.5 us -> 16.6 us
  waiting for transfers between devices: 17.4 us -> 15.3 us
    psum x1 -> x0, blocking collectives: 30.1 us -> none  [per_device(): lax.psum(upward.astype(jnp.bfloat16), 'col').astype(jnp.float32)]
    all_gather x0 -> x1, blocking collectives: none -> 22 us  [per_device(): lax.all_gather(upward.astype(jnp.bfloat16), 'col')]
    ppermute x2, waiting for transfers between devices: 0.01 us -> 4.88 us  [padded_2(): lax.ppermute(tail, axis, [(i, (i + 1) % count) for i in range(count)])]
    ppermute x2, waiting for transfers between devices: 13.2 us -> 8.46 us  [padded_2(): lax.ppermute(head, axis, [((i + 1) % count, i) for i in range(count)])]
    all_gather x1, blocking collectives: 12.6 us -> 9.78 us  [per_device(): lax.all_gather(own_region[None].astype(jnp.bfloat16), 'row', axis=0, tile...]
    ppermute x4, starting transfers between devices: 3.15 us -> 5.56 us  [from_behind(): return lax.ppermute(value, axis, pairs)]
    ppermute x4, waiting for transfers between devices: 4.15 us -> 1.98 us  [from_behind(): return lax.ppermute(value, axis, pairs)]
    ppermute x2, starting transfers between devices: 7.24 us -> 8.77 us  [padded_2(): lax.ppermute(head, axis, [((i + 1) % count, i) for i in range(count)])]
  transfers between devices with their start and end apart: 8 -> 8, of which waited for: 3 -> 4; matrix products, arithmetic and copies ran while one was open for 8% -> 7% of each run, Pallas kernels for 0% -> 0%
where the time goes in v1:
time: 103 us
  blocking collectives  57.8 us (56%)
  starting transfers between devices  16.6 us (16%)
  waiting for transfers between devices  15.3 us (15%)
  matrix products  7.13 us (7%)
  other arithmetic  2.89 us (3%)
  local copies, waits for them, and re-layouts  2.3 us (2%)
    all_gather x1, blocking collectives, per_device(): lax.all_gather(three_rows[:, None].astype(jnp.bfloat16), 'col', axis=1, t...  26 us
    all_gather x1, blocking collectives, per_device(): lax.all_gather(upward.astype(jnp.bfloat16), 'col')  22 us
    all_gather x1, blocking collectives, per_device(): lax.all_gather(own_region[None].astype(jnp.bfloat16), 'row', axis=0, tile...  9.78 us
    ppermute x2, starting transfers between devices, padded_2(): lax.ppermute(head, axis, [((i + 1) % count, i) for i in range(count)])  8.77 us
    ppermute x2, waiting for transfers between devices, padded_2(): lax.ppermute(head, axis, [((i + 1) % count, i) for i in range(count)])  8.46 us
    ppermute x4, starting transfers between devices, from_behind(): return lax.ppermute(value, axis, pairs)  5.56 us
    ppermute x2, waiting for transfers between devices, padded_2(): lax.ppermute(tail, axis, [(i, (i + 1) % count) for i in range(count)])  4.88 us
    ppermute x2, starting transfers between devices, padded_2(): lax.ppermute(tail, axis, [(i, (i + 1) % count) for i in range(count)])  2.25 us
  transfers between devices with their start and end apart: 8, of which 4 were waited for; matrix products, arithmetic and copies ran while one was open for 7% of the time, Pallas kernels for 0%

profile of v1, /device:TPU:1, one launch (start us, length us, event | category | flops | bytes accessed | tf_op | source)
XLA Modules:
  0.0 102.8 jit_solution(4839369964947182886)
XLA Ops:
  0.0 0.0 copy-start
  0.0 0.0 copy-start.4
  0.0 0.0 copy-start.3
  0.0 0.1 collective-permute-start
  0.1 1.2 %fusion.36 = (bf16[128,64]{0,1:T(8,128)(2,1)S(1)}, f32[128,64]{0,1:T(8,128)S(1)}) fusion(bf16[1,1,64,384]{3,2,1,0:T(8,128)(2,1)} %param.15, bf16[1,1,128,384]{3,2,1,0:T(8,128)(2,1)} %param.11), kind=kOutput, calls=%fused_computation.64 | convolution fusion | flops 6299648 | bytes 196608 | tf_op jit(solution)/shard_map/dot_general | solution.py:54
  1.3 2.7 %collective-permute-start.7 = (bf16[128,64]{0,1:T(8,128)(2,1)S(1)}, bf16[128,64]{0,1:T(8,128)(2,1)S(1)}, u32[]{:S(2)}, u32[]{:S(2)}) collective-permute-start(bf16[128,64]{0,1:T(8,128)(2,1)S(1)} %get-tuple-element.7), channel_id=1, source_target_pairs={{0,16},{8,24},{16,0},{24,8},{1,17},{9,25},{17,1},{25,9},{2,18},{10... | collective-permute-start | bytes 49160 | tf_op jit(solution)/shard_map/ppermute | solution.py:10
  4.0 0.4 collective-permute-start.6
  4.4 0.7 fusion.29
  5.7 0.7 compare_and_fusion.1
  6.3 0.9 convolution_convert_fusion
  7.3 22.0 %all-gather = bf16[1024,64]{0,1:T(8,128)(2,1)S(1)} all-gather(bf16[128,64]{0,1:T(8,128)(2,1)S(1)} %convolution_convert_fusion), channel_id=2, replica_groups=mesh['row'=4,'col'=8] {'col'}, dimensions={0}, use_global_device_ids=true | all-gather | bytes 147456 | tf_op jit(solution)/shard_map/all_gather | solution.py:74
  29.3 0.1 bitcast_reduce_fusion
  29.4 9.8 %all-gather.1 = bf16[512,64]{0,1:T(8,128)(2,1)S(1)} all-gather(bf16[128,64]{0,1:T(8,128)(2,1)S(1)} %bitcast_reduce_fusion), channel_id=3, replica_groups=mesh['row'=4,'col'=8] {'row'}, dimensions={0}, use_global_device_ids=true | all-gather | bytes 81920 | tf_op jit(solution)/shard_map/all_gather | solution.py:77
  39.2 0.7 fusion.30
  39.9 0.7 compare_and_fusion
  40.6 0.6 gather_fusion.1
  41.1 1.1 %convolution_bitcast_fusion = f32[128,64]{0,1:T(8,128)S(1)} fusion(f32[4,128,64]{1,2,0:T(8,128)S(1)} %gather_fusion.1, bf16[1,4,64,64]{3,2,1,0:T(8,128)(2,1)} %param.18, f32[4]{0:T(128)S(1)} %get-tuple-element.6, pred[4]{0:T(512)(128)(4,1)S(1)} %get-tuple-element.5), kind=kOutput, calls=%fused_computation.9 | convolution fusion | flops 25231360 | bytes 196628 | tf_op jit(solution)/shard_map/fvk,fkl->vl/dot_general | solution.py:83
  42.3 0.0 collective-permute-done
  42.3 2.4 %collective-permute-start.1 = (bf16[1,1,128,384]{3,2,1,0:T(8,128)(2,1)S(1)}, bf16[1,1,128,384]{3,2,1,0:T(8,128)(2,1)S(1)}, u32[]{:S(2)}, u32[]{:S(2)}) collective-permute-start(bf16[1,1,128,384]{3,2,1,0:T(8,128)(2,1)S(1)} %collective-permute-done), channel_id=1, source_target_pairs={{0,7},{1,0},{2,1},{3,2},{4,3},{5,4},{6,5},{7,6},{8,15},{9,8},{10,9... | collective-permute-start | bytes 294920 | tf_op jit(solution)/shard_map/ppermute | solution.py:10
  44.7 0.0 collective-permute-done.7
  44.7 0.0 collective-permute-done.6
  44.7 2.0 %collective-permute-done.1 = bf16[1,1,128,384]{3,2,1,0:T(8,128)(2,1)S(1)} collective-permute-done((bf16[1,1,128,384]{3,2,1,0:T(8,128)(2,1)S(1)}, bf16[1,1,128,384]{3,2,1,0:T(8,128)(2,1)S(1)}, u32[]{:S(2)}, u32[]{:S(2)}) %collective-permute-start.1) | collective-permute-done | bytes 98336 | tf_op jit(solution)/shard_map/ppermute | solution.py:10
  46.7 2.2 %collective-permute-start.2 = (bf16[1,1,128,384]{3,2,1,0:T(8,128)(2,1)S(1)}, bf16[1,1,128,384]{3,2,1,0:T(8,128)(2,1)S(1)}, u32[]{:S(2)}, u32[]{:S(2)}) collective-permute-start(bf16[1,1,128,384]{3,2,1,0:T(8,128)(2,1)S(1)} %collective-permute-done.1), channel_id=1, source_target_pairs={{0,8},{8,16},{16,24},{24,0},{1,9},{9,17},{17,25},{25,1},{2,10},{10... | collective-permute-start | bytes 294920 | tf_op jit(solution)/shard_map/ppermute | solution.py:20
  48.9 26.0 %all_gather.12 = bf16[3,8,128,64]{2,3,1,0:T(8,128)(2,1)S(1)} all-gather(bf16[3,1,128,64]{2,3,1,0:T(8,128)(2,1)S(1)} %pad_maximum_fusion.1), channel_id=1, replica_groups=mesh['row'=4,'col'=8] {'col'}, dimensions={1}, use_global_device_ids=true | all-gather | bytes 442368 | tf_op jit(solution)/shard_map/all_gather | solution.py:64
  74.9 4.3 %collective-permute-start.3 = (bf16[1,1,128,384]{3,2,1,0:T(8,128)(2,1)S(1)}, bf16[1,1,128,384]{3,2,1,0:T(8,128)(2,1)S(1)}, u32[]{:S(2)}, u32[]{:S(2)}) collective-permute-start(bf16[1,1,128,384]{3,2,1,0:T(8,128)(2,1)S(1)} %collective-permute-done.1), channel_id=1, source_target_pairs={{8,0},{16,8},{24,16},{0,24},{9,1},{17,9},{25,17},{1,25},{10,2},{18... | collective-permute-start | bytes 294920 | tf_op jit(solution)/shard_map/ppermute | solution.py:22
  79.2 0.0 collective-permute-done.2
  79.3 3.5 %collective-permute-done.3 = bf16[1,1,128,384]{3,2,1,0:T(8,128)(2,1)S(1)} collective-permute-done((bf16[1,1,128,384]{3,2,1,0:T(8,128)(2,1)S(1)}, bf16[1,1,128,384]{3,2,1,0:T(8,128)(2,1)S(1)}, u32[]{:S(2)}, u32[]{:S(2)}) %collective-permute-start.3) | collective-permute-done | bytes 98336 | tf_op jit(solution)/shard_map/ppermute | solution.py:22
  82.8 4.5 %collective-permute-start.5 = (bf16[3,1,128,384]{3,2,1,0:T(8,128)(2,1)S(1)}, bf16[3,1,128,384]{3,2,1,0:T(8,128)(2,1)S(1)}, u32[]{:S(2)}, u32[]{:S(2)}) collective-permute-start(bf16[3,1,128,384]{3,2,1,0:T(8,128)(2,1)S(1)} %constant_dynamic-update-slice_fusion), channel_id=1, source_target_pairs={{1,0},{2,1},{3,2},{4,3},{5,4},{6,5},{7,6},{0,7},{9,8},{10,9},{11,1... | collective-permute-start | bytes 884744 | tf_op jit(solution)/shard_map/ppermute | solution.py:22
  87.3 0.0 collective-permute-start.4
  87.3 0.0 copy-done.4
  87.3 0.3 convolution_bitcast_fusion.1
  87.5 0.0 copy-done.3
  87.6 0.8 convolution_add_fusion.1
  88.4 4.9 %collective-permute-done.5 = bf16[3,1,128,384]{3,2,1,0:T(8,128)(2,1)S(1)} collective-permute-done((bf16[3,1,128,384]{3,2,1,0:T(8,128)(2,1)S(1)}, bf16[3,1,128,384]{3,2,1,0:T(8,128)(2,1)S(1)}, u32[]{:S(2)}, u32[]{:S(2)}) %collective-permute-start.5) | collective-permute-done | bytes 294944 | tf_op jit(solution)/shard_map/ppermute | solution.py:22
  93.3 4.9 %collective-permute-done.4 = bf16[3,1,128,384]{3,2,1,0:T(8,128)(2,1)S(1)} collective-permute-done((bf16[3,1,128,384]{3,2,1,0:T(8,128)(2,1)S(1)}, bf16[3,1,128,384]{3,2,1,0:T(8,128)(2,1)S(1)}, u32[]{:S(2)}, u32[]{:S(2)}) %collective-permute-start.4) | collective-permute-done | bytes 294944 | tf_op jit(solution)/shard_map/ppermute | solution.py:20
  98.2 0.1 pad_maximum_fusion
  98.3 1.7 %gather_fusion = bf16[9,128,384]{2,1,0:T(8,128)(2,1)} fusion(bf16[9,128,384]{2,1,0:T(8,128)(2,1)S(1)} %bitcast.74, s32[1024]{0:T(1024)S(1)} %pad_clamp_fusion.1), kind=kCustom, calls=%fused_computation | custom fusion | bytes 1769508 | tf_op jit(solution)/shard_map/jit(_take)/gather | solution.py:47
  100.0 0.0 copy-start.1
  100.0 0.0 copy-start.2
  100.0 0.0 copy-done
  100.0 1.9 %fusion.2 = f32[128,384]{1,0:T(8,128)S(1)} fusion(bf16[1,1,9,384,384]{4,3,2,1,0:T(8,128)(2,1)S(1)} %copy-done, bf16[9,128,384]{2,1,0:T(8,128)(2,1)} %gather_fusion, pred[9]{0:T(512)(128)(4,1)S(1)} %get-tuple-element.9, pred[9]{0:T(512)(128)(4,1)S(1)} %get-tuple-element.10), kind=kOutput, calls=%fused_computation.5 | convolution fusion | flops 340623360 | bytes 3735570 | tf_op jit(solution)/shard_map/svp,spq->vq/dot_general | solution.py:51
  101.8 0.0 copy-done.1
  101.9 0.0 copy-done.2
  101.9 0.9 fusion.6
  (8 shorter events, 0.1 us)
Async XLA Ops:
  0.0 100.0 %copy-start = (bf16[1,1,9,384,384]{4,3,2,1,0:T(8,128)(2,1)S(1)}, bf16[1,1,9,384,384]{4,3,2,1,0:T(8,128)(2,1)}, u32[]{:S(2)}) copy-start(bf16[1,1,9,384,384]{4,3,2,1,0:T(8,128)(2,1)} %param.12) | copy-start | bytes 7962628
  0.0 87.3 %copy-start.4 = (bf16[1,1,3,5,64,64]{5,4,3,2,1,0:T(8,128)(2,1)S(1)}, bf16[1,1,3,5,64,64]{5,4,3,2,1,0:T(8,128)(2,1)}, u32[]{:S(2)}) copy-start(bf16[1,1,3,5,64,64]{5,4,3,2,1,0:T(8,128)(2,1)} %param.17) | copy-start | bytes 368644
  0.0 87.5 %copy-start.3 = (bf16[1,1,64,64]{3,2,1,0:T(8,128)(2,1)S(1)}, bf16[1,1,64,64]{3,2,1,0:T(8,128)(2,1)}, u32[]{:S(2)}) copy-start(bf16[1,1,64,64]{3,2,1,0:T(8,128)(2,1)} %param.20) | copy-start | bytes 24580
  0.0 42.3 %collective-permute-start = (bf16[1,1,128,384]{3,2,1,0:T(8,128)(2,1)}, bf16[1,1,128,384]{3,2,1,0:T(8,128)(2,1)S(1)}, u32[]{:S(2)}, u32[]{:S(2)}) collective-permute-start(bf16[1,1,128,384]{3,2,1,0:T(8,128)(2,1)} %param.11), channel_id=1, source_target_pairs={{0,24},{8,0},{16,8},{24,16},{1,25},{9,1},{17,9},{25,17},{2,26},{10... | collective-permute-start | bytes 294920 | tf_op jit(solution)/shard_map/ppermute | solution.py:10
  1.3 43.4 %collective-permute-start.7 = (bf16[128,64]{0,1:T(8,128)(2,1)S(1)}, bf16[128,64]{0,1:T(8,128)(2,1)S(1)}, u32[]{:S(2)}, u32[]{:S(2)}) collective-permute-start(bf16[128,64]{0,1:T(8,128)(2,1)S(1)} %get-tuple-element.7), channel_id=1, source_target_pairs={{0,16},{8,24},{16,0},{24,8},{1,17},{9,25},{17,1},{25,9},{2,18},{10... | collective-permute-start | bytes 49160 | tf_op jit(solution)/shard_map/ppermute | solution.py:10
  4.0 40.7 %collective-permute-start.6 = (bf16[128,64]{0,1:T(8,128)(2,1)S(1)}, bf16[128,64]{0,1:T(8,128)(2,1)S(1)}, u32[]{:S(2)}, u32[]{:S(2)}) collective-permute-start(bf16[128,64]{0,1:T(8,128)(2,1)S(1)} %get-tuple-element.7), channel_id=1, source_target_pairs={{0,24},{8,0},{16,8},{24,16},{1,25},{9,1},{17,9},{25,17},{2,26},{10... | collective-permute-start | bytes 49160 | tf_op jit(solution)/shard_map/ppermute | solution.py:10
  42.3 4.4 %collective-permute-start.1 = (bf16[1,1,128,384]{3,2,1,0:T(8,128)(2,1)S(1)}, bf16[1,1,128,384]{3,2,1,0:T(8,128)(2,1)S(1)}, u32[]{:S(2)}, u32[]{:S(2)}) collective-permute-start(bf16[1,1,128,384]{3,2,1,0:T(8,128)(2,1)S(1)} %collective-permute-done), channel_id=1, source_target_pairs={{0,7},{1,0},{2,1},{3,2},{4,3},{5,4},{6,5},{7,6},{8,15},{9,8},{10,9... | collective-permute-start | bytes 294920 | tf_op jit(solution)/shard_map/ppermute | solution.py:10
  46.7 32.5 %collective-permute-start.2 = (bf16[1,1,128,384]{3,2,1,0:T(8,128)(2,1)S(1)}, bf16[1,1,128,384]{3,2,1,0:T(8,128)(2,1)S(1)}, u32[]{:S(2)}, u32[]{:S(2)}) collective-permute-start(bf16[1,1,128,384]{3,2,1,0:T(8,128)(2,1)S(1)} %collective-permute-done.1), channel_id=1, source_target_pairs={{0,8},{8,16},{16,24},{24,0},{1,9},{9,17},{17,25},{25,1},{2,10},{10... | collective-permute-start | bytes 294920 | tf_op jit(solution)/shard_map/ppermute | solution.py:20
  74.9 7.9 %collective-permute-start.3 = (bf16[1,1,128,384]{3,2,1,0:T(8,128)(2,1)S(1)}, bf16[1,1,128,384]{3,2,1,0:T(8,128)(2,1)S(1)}, u32[]{:S(2)}, u32[]{:S(2)}) collective-permute-start(bf16[1,1,128,384]{3,2,1,0:T(8,128)(2,1)S(1)} %collective-permute-done.1), channel_id=1, source_target_pairs={{8,0},{16,8},{24,16},{0,24},{9,1},{17,9},{25,17},{1,25},{10,2},{18... | collective-permute-start | bytes 294920 | tf_op jit(solution)/shard_map/ppermute | solution.py:22
  82.8 10.5 %collective-permute-start.5 = (bf16[3,1,128,384]{3,2,1,0:T(8,128)(2,1)S(1)}, bf16[3,1,128,384]{3,2,1,0:T(8,128)(2,1)S(1)}, u32[]{:S(2)}, u32[]{:S(2)}) collective-permute-start(bf16[3,1,128,384]{3,2,1,0:T(8,128)(2,1)S(1)} %constant_dynamic-update-slice_fusion), channel_id=1, source_target_pairs={{1,0},{2,1},{3,2},{4,3},{5,4},{6,5},{7,6},{0,7},{9,8},{10,9},{11,1... | collective-permute-start | bytes 884744 | tf_op jit(solution)/shard_map/ppermute | solution.py:22
  87.3 10.9 %collective-permute-start.4 = (bf16[3,1,128,384]{3,2,1,0:T(8,128)(2,1)S(1)}, bf16[3,1,128,384]{3,2,1,0:T(8,128)(2,1)S(1)}, u32[]{:S(2)}, u32[]{:S(2)}) collective-permute-start(bf16[3,1,128,384]{3,2,1,0:T(8,128)(2,1)S(1)} %constant_dynamic-update-slice_fusion), channel_id=1, source_target_pairs={{0,1},{1,2},{2,3},{3,4},{4,5},{5,6},{6,7},{7,0},{8,9},{9,10},{10,1... | collective-permute-start | bytes 884744 | tf_op jit(solution)/shard_map/ppermute | solution.py:20
  100.0 1.9 %copy-start.1 = (f32[128,64]{0,1:T(8,128)S(1)}, f32[128,64]{0,1:T(8,128)}, u32[]{:S(2)}) copy-start(f32[128,64]{0,1:T(8,128)} %convolution_add_fusion.1) | copy-start | bytes 98308
  100.0 1.9 %copy-start.2 = (bf16[1,1,64,384]{3,2,1,0:T(8,128)(2,1)S(1)}, bf16[1,1,64,384]{3,2,1,0:T(8,128)(2,1)}, u32[]{:S(2)}) copy-start(bf16[1,1,64,384]{3,2,1,0:T(8,128)(2,1)} %param.21) | copy-start | bytes 147460
